TPU v7x, 32 devices: a whole 2x2x4 slice. The times are simulated.
32 devices in a mesh: tm: 4 (over x, core), anta: 4 (over z), antb: 2 (over y).
Axes of the slice: x: 2, y: 2, z: 4, core: 2. Of those that a mesh axis runs over, the one named last changes fastest.
Arguments:
- samples: bfloat16 [2, 512, 6144], P('antb', 'anta', 'tm'), may hold values from -6 to 6
Outputs:
- correlation: float32 [256, 2, 512, 2, 512], P('tm', None, 'anta', 'antb')
All inputs are finite; a program needn't handle non-finite values.
Results may differ from a plain program's by a relative error of at most 0.0003.
Values may be sent and summed in bfloat16 or wider, within the bound.
A program may use at most 128 MiB of HBM per device.

v0:
```python
import math
import jax
import jax.numpy as jnp
from jax import lax
from jax.sharding import PartitionSpec as P

ANTENNA_COUNT = 512
POLARISATION_NUM = 2
LAG_TOTAL = 256


def lag_terms(row_padded, columns, lag_start, lag_count, window_len):
    group_len = math.gcd(lag_count, 8)
    flat_cols = columns.reshape(columns.shape[1], columns.shape[2])

    def one_group(group_index):
        first_lag = lag_start + group_index * group_len
        pieces = [
            lax.dynamic_slice_in_dim(row_padded, LAG_TOTAL - first_lag - step_index, window_len, 1)
            for step_index in range(group_len)
        ]
        stacked = jnp.stack(pieces, 0)
        return jnp.einsum("kit,jt->kij", stacked, flat_cols, preferred_element_type=jnp.float32)

    grouped = lax.map(one_group, jnp.arange(lag_count // group_len, dtype=jnp.int32))
    return grouped.reshape(lag_count, row_padded.shape[0], flat_cols.shape[0])


def collect_rows(own_window):
    return lax.all_gather(own_window, "antb", axis=0, tiled=True)


def per_device(samples):
    antenna_total = samples.shape[1]
    block_len = samples.shape[2]
    tm_size = lax.axis_size("tm")
    lag_portion = LAG_TOTAL // tm_size
    full_length = block_len * tm_size
    factor = 1.0 / math.sqrt(full_length)
    lag_start = lax.axis_index("tm") * lag_portion
    col_tiles = lax.all_gather(samples, "anta", axis=1, tiled=True)
    columns = lax.all_gather(col_tiles, "tm", axis=2, tiled=True)
    own_rows = lax.dynamic_slice_in_dim(
        columns, lax.axis_index("anta") * antenna_total, antenna_total, 1
    )
    row_samples = collect_rows(own_rows)
    row_padded = jnp.pad(
        row_samples.reshape(POLARISATION_NUM * antenna_total, full_length), ((0, 0), (LAG_TOTAL, 0))
    )
    lag_group_block = lag_terms(row_padded, columns, lag_start, lag_portion, full_length)
    accumulated_sum = lag_group_block.reshape(
        lag_portion, POLARISATION_NUM, antenna_total, 1, ANTENNA_COUNT
    )
    return accumulated_sum * factor


def solution(mesh):
    return jax.shard_map(
        per_device,
        mesh=mesh,
        in_specs=(P("antb", "anta", "tm"),),
        out_specs=P("tm", None, "anta", "antb", None),
        check_vma=False,
    )
```

profile of v0, /device:TPU:0, one launch (start us, length us, event | category | flops | bytes accessed | tf_op | source)
XLA Modules:
  0.0 584.9 jit_solution(11511170079034413192)
XLA Ops:
  7.3 41.4 %all-gather.4.cloned.1.call-done = bf16[1,512,1536]{2,1,0:T(8,128)(2,1)} async-done(((bf16[1,128,1536]{2,1,0:T(8,128)(2,1)}), bf16[1,512,1536]{2,1,0:T(8,128)(2,1)}) %all-gather.4.cloned.1.call-update) | async-done | bytes 1572880 | tf_op jit(solution)/shard_map/all_gather | solution.py:41
  48.8 46.7 %all-gather.6.cloned.1.call-done = bf16[1,512,6144]{2,1,0:T(8,128)(2,1)} async-done(((bf16[1,512,1536]{2,1,0:T(8,128)(2,1)}), bf16[1,512,6144]{2,1,0:T(8,128)(2,1)}) %all-gather.6.cloned.1.call-update) | async-done | bytes 6291472 | tf_op jit(solution)/shard_map/all_gather | solution.py:42
  98.2 45.1 %all-gather.8.cloned.1.call-done = bf16[2,128,6144]{2,1,0:T(8,128)(2,1)} async-done(((bf16[1,128,6144]{2,1,0:T(8,128)(2,1)}), bf16[2,128,6144]{2,1,0:T(8,128)(2,1)}) %all-gather.8.cloned.1.call-update) | async-done | bytes 3145744 | tf_op jit(solution)/shard_map/all_gather | solution.py:30
  145.4 360.6 %while.14 = (s32[]{:T(128)}, f32[8,8,256,512]{3,2,1,0:T(8,128)}, s32[8]{0:T(128)S(1)}, s32[]{:T(128)}, bf16[256,6400]{1,0:T(8,128)(2,1)S(1)}, /*index=5*/bf16[51...) while((s32[]{:T(128)}, f32[8,8,256,512]{3,2,1,0:T(8,128)}, ...), condition=%wide.region_1.2_spmd, body=%wide.region_0.1_spmd.sunk | while | flops 12884901888 | bytes 85984392 | solution.py:25
  149.5 2.9 bitcast_dynamic-update-slice_fusion.19
  152.4 2.9 bitcast_dynamic-update-slice_fusion.20
  169.4 21.0 %bitcast_dynamic-update-slice_fusion.26 = f32[8,8,256,512]{3,2,1,0:T(8,128)} fusion(f32[8,8,256,512]{3,2,1,0:T(8,128)} %get-tuple-element.216, s32[]{:T(128)} %get-tuple-element.215, bf16[8,256,6144]{2,1,0:T(8,128)(2,1)} %bitcast_dynamic-update-slice_fusion.25, bf16[512,6144]{1,0:T(8,128)(2,1)} %get-tuple-element.245), kind=kOutput, calls=%fused_computation.2.clone.1 | convolution fusion | flops 12884901888 | bytes 35652096 | tf_op jit(solution)/shard_map/while/body/eval_jaxpr/kit,jt->kij/dot_general | solution.py:23
  194.6 2.9 bitcast_dynamic-update-slice_fusion.19
  197.5 2.9 bitcast_dynamic-update-slice_fusion.20
  214.5 21.1 %bitcast_dynamic-update-slice_fusion.26 = f32[8,8,256,512]{3,2,1,0:T(8,128)} fusion(f32[8,8,256,512]{3,2,1,0:T(8,128)} %get-tuple-element.216, s32[]{:T(128)} %get-tuple-element.215, bf16[8,256,6144]{2,1,0:T(8,128)(2,1)} %bitcast_dynamic-update-slice_fusion.25, bf16[512,6144]{1,0:T(8,128)(2,1)} %get-tuple-element.245), kind=kOutput, calls=%fused_computation.2.clone.1 | convolution fusion | flops 12884901888 | bytes 35652096 | tf_op jit(solution)/shard_map/while/body/eval_jaxpr/kit,jt->kij/dot_general | solution.py:23
  242.6 2.9 bitcast_dynamic-update-slice_fusion.20
  259.6 21.1 %bitcast_dynamic-update-slice_fusion.26 = f32[8,8,256,512]{3,2,1,0:T(8,128)} fusion(f32[8,8,256,512]{3,2,1,0:T(8,128)} %get-tuple-element.216, s32[]{:T(128)} %get-tuple-element.215, bf16[8,256,6144]{2,1,0:T(8,128)(2,1)} %bitcast_dynamic-update-slice_fusion.25, bf16[512,6144]{1,0:T(8,128)(2,1)} %get-tuple-element.245), kind=kOutput, calls=%fused_computation.2.clone.1 | convolution fusion | flops 12884901888 | bytes 35652096 | tf_op jit(solution)/shard_map/while/body/eval_jaxpr/kit,jt->kij/dot_general | solution.py:23
  287.6 2.9 bitcast_dynamic-update-slice_fusion.20
  304.7 21.1 %bitcast_dynamic-update-slice_fusion.26 = f32[8,8,256,512]{3,2,1,0:T(8,128)} fusion(f32[8,8,256,512]{3,2,1,0:T(8,128)} %get-tuple-element.216, s32[]{:T(128)} %get-tuple-element.215, bf16[8,256,6144]{2,1,0:T(8,128)(2,1)} %bitcast_dynamic-update-slice_fusion.25, bf16[512,6144]{1,0:T(8,128)(2,1)} %get-tuple-element.245), kind=kOutput, calls=%fused_computation.2.clone.1 | convolution fusion | flops 12884901888 | bytes 35652096 | tf_op jit(solution)/shard_map/while/body/eval_jaxpr/kit,jt->kij/dot_general | solution.py:23
  332.7 2.9 bitcast_dynamic-update-slice_fusion.20
  349.7 21.1 %bitcast_dynamic-update-slice_fusion.26 = f32[8,8,256,512]{3,2,1,0:T(8,128)} fusion(f32[8,8,256,512]{3,2,1,0:T(8,128)} %get-tuple-element.216, s32[]{:T(128)} %get-tuple-element.215, bf16[8,256,6144]{2,1,0:T(8,128)(2,1)} %bitcast_dynamic-update-slice_fusion.25, bf16[512,6144]{1,0:T(8,128)(2,1)} %get-tuple-element.245), kind=kOutput, calls=%fused_computation.2.clone.1 | convolution fusion | flops 12884901888 | bytes 35652096 | tf_op jit(solution)/shard_map/while/body/eval_jaxpr/kit,jt->kij/dot_general | solution.py:23
  377.8 2.9 bitcast_dynamic-update-slice_fusion.20
  394.8 21.1 %bitcast_dynamic-update-slice_fusion.26 = f32[8,8,256,512]{3,2,1,0:T(8,128)} fusion(f32[8,8,256,512]{3,2,1,0:T(8,128)} %get-tuple-element.216, s32[]{:T(128)} %get-tuple-element.215, bf16[8,256,6144]{2,1,0:T(8,128)(2,1)} %bitcast_dynamic-update-slice_fusion.25, bf16[512,6144]{1,0:T(8,128)(2,1)} %get-tuple-element.245), kind=kOutput, calls=%fused_computation.2.clone.1 | convolution fusion | flops 12884901888 | bytes 35652096 | tf_op jit(solution)/shard_map/while/body/eval_jaxpr/kit,jt->kij/dot_general | solution.py:23
  422.9 2.9 bitcast_dynamic-update-slice_fusion.20
  439.9 21.1 %bitcast_dynamic-update-slice_fusion.26 = f32[8,8,256,512]{3,2,1,0:T(8,128)} fusion(f32[8,8,256,512]{3,2,1,0:T(8,128)} %get-tuple-element.216, s32[]{:T(128)} %get-tuple-element.215, bf16[8,256,6144]{2,1,0:T(8,128)(2,1)} %bitcast_dynamic-update-slice_fusion.25, bf16[512,6144]{1,0:T(8,128)(2,1)} %get-tuple-element.245), kind=kOutput, calls=%fused_computation.2.clone.1 | convolution fusion | flops 12884901888 | bytes 35652096 | tf_op jit(solution)/shard_map/while/body/eval_jaxpr/kit,jt->kij/dot_general | solution.py:23
  467.9 2.9 bitcast_dynamic-update-slice_fusion.20
  485.0 21.1 %bitcast_dynamic-update-slice_fusion.26 = f32[8,8,256,512]{3,2,1,0:T(8,128)} fusion(f32[8,8,256,512]{3,2,1,0:T(8,128)} %get-tuple-element.216, s32[]{:T(128)} %get-tuple-element.215, bf16[8,256,6144]{2,1,0:T(8,128)(2,1)} %bitcast_dynamic-update-slice_fusion.25, bf16[512,6144]{1,0:T(8,128)(2,1)} %get-tuple-element.245), kind=kOutput, calls=%fused_computation.2.clone.1 | convolution fusion | flops 12884901888 | bytes 35652096 | tf_op jit(solution)/shard_map/while/body/eval_jaxpr/kit,jt->kij/dot_general | solution.py:23
  506.0 23.9 %broadcast_multiply_fusion = f32[8,8,256,512]{3,2,1,0:T(8,128)} fusion(f32[8,8,256,512]{3,2,1,0:T(8,128)} %get-tuple-element.140), kind=kLoop, calls=%fused_computation.11 | loop fusion | flops 8388608 | bytes 67108864 | tf_op jit(solution)/shard_map/mul | solution.py:54
  530.0 48.4 %mul.39 = f32[64,2,128,1,512]{4,3,2,1,0:T(1,128)} reshape(f32[8,8,256,512]{3,2,1,0:T(8,128)} %broadcast_multiply_fusion) | data formatting | bytes 67108864 | tf_op jit(solution)/shard_map/mul | solution.py:54
  (72 shorter events, 163.9 us)
Async XLA Ops:
  6.5 42.1 %all-gather.4.cloned.1.call-start = ((), (), s32[]{:S(2)}) async-start(), calls=%async_computation | async-start | bytes 1966080 | tf_op jit(solution)/shard_map/all_gather | solution.py:41
  7.3 88.2 %all-gather.6.cloned.1.call-start = ((), (), s32[]{:S(2)}) async-start(), calls=%async_computation.1 | async-start | bytes 7864320 | tf_op jit(solution)/shard_map/all_gather | solution.py:42
  48.7 94.6 %all-gather.8.cloned.1.call-start = ((), (), s32[]{:S(2)}) async-start(), calls=%async_computation.2 | async-start | bytes 4718592 | tf_op jit(solution)/shard_map/all_gather | solution.py:30
Sparse Core Ops, SparseCore 0:
  8.9 39.7 all-gather.3
  50.2 45.2 all-gather.5
  98.3 44.9 all-gather.7
where the time goes:
time: 586 us; the launch traced here: 585 us
  local copies, waits for them, and re-layouts  240 us (41%)
  matrix products  168 us (29%)
  waiting for transfers between devices  134 us (23%)
  other arithmetic  23.9 us (4%)
  between operations  13.1 us (2%)
    dot_general x8, matrix products, one_group(): jnp.einsum('kit,jt->kij', stacked, flat_cols, preferred_element_type=jnp....  168 us
    while x56, local copies, waits for them, and re-layouts  159 us
    mul x1, local copies, waits for them, and re-layouts, per_device(): return accumulated_sum * factor  48.4 us
    all_gather x1, waiting for transfers between devices, per_device(): columns = lax.all_gather(col_tiles, 'tm', axis=2, tiled=True)  46.7 us
    all_gather x1, waiting for transfers between devices, collect_rows(): return lax.all_gather(own_window, 'antb', axis=0, tiled=True)  45.1 us
    all_gather x1, waiting for transfers between devices, per_device(): col_tiles = lax.all_gather(samples, 'anta', axis=1, tiled=True)  41.4 us
    mul x1, other arithmetic, per_device(): return accumulated_sum * factor  23.9 us
    another operation x8, local copies, waits for them, and re-layouts, one_group(): stacked = jnp.stack(pieces, 0)  22.7 us
  transfers between devices with their start and end apart: 3, of which 3 were waited for; matrix products, arithmetic and copies ran while one was open for 0% of the time, Pallas kernels for 0%

commit v1 on v0

--- a/solution.py
+++ b/solution.py
@@ -3,6 +3,7 @@
 import jax.numpy as jnp
 from jax import lax
 from jax.sharding import PartitionSpec as P
+from jax.lax import all_to_all, axis_size
 
 ANTENNA_COUNT = 512
 POLARISATION_NUM = 2
@@ -39,7 +40,10 @@
     factor = 1.0 / math.sqrt(full_length)
     lag_start = lax.axis_index("tm") * lag_portion
     col_tiles = lax.all_gather(samples, "anta", axis=1, tiled=True)
-    columns = lax.all_gather(col_tiles, "tm", axis=2, tiled=True)
+    columns = jnp.concatenate(
+        all_to_all(jnp.stack([col_tiles for _ in range(axis_size("tm"))], axis=0), "tm", 0, 0),
+        axis=2,
+    )
     own_rows = lax.dynamic_slice_in_dim(
         columns, lax.axis_index("anta") * antenna_total, antenna_total, 1
     )

time: 586 us -> 629 us (1.073)
  local copies, waits for them, and re-layouts: 240 us -> 263 us
  waiting for transfers between devices: 134 us -> 147 us
    all_to_all x0 -> x1, waiting for transfers between devices: none -> 70.6 us  [per_device(): all_to_all(jnp.stack([col_tiles for _ in range(axis_size('tm'))], axis=0)...]
    all_gather x1 -> x0, waiting for transfers between devices: 46.7 us -> none  [per_device(): columns = lax.all_gather(col_tiles, 'tm', axis=2, tiled=True)]
    all_gather x1, waiting for transfers between devices: 45.1 us -> 34.2 us  [collect_rows(): return lax.all_gather(own_window, 'antb', axis=0, tiled=True)]
    while x56 -> x57, local copies, waits for them, and re-layouts: 159 us -> 168 us
    all_to_all x0 -> x1, local copies, waits for them, and re-layouts: none -> 8.65 us  [per_device(): all_to_all(jnp.stack([col_tiles for _ in range(axis_size('tm'))], axis=0)...]
  transfers between devices with their start and end apart: 3 -> 3, of which waited for: 3 -> 3; matrix products, arithmetic and copies ran while one was open for 0% -> 1% of each run, Pallas kernels for 0% -> 0%
where the time goes in v1:
time: 629 us; the launch traced here: 627 us
  local copies, waits for them, and re-layouts  263 us (42%)
  matrix products  168 us (27%)
  waiting for transfers between devices  147 us (23%)
  other arithmetic  23.9 us (4%)
  between operations  13.4 us (2%)
    dot_general x8, matrix products, one_group(): jnp.einsum('kit,jt->kij', stacked, flat_cols, preferred_element_type=jnp....  168 us
    while x56, local copies, waits for them, and re-layouts  159 us
    all_to_all x1, waiting for transfers between devices, per_device(): all_to_all(jnp.stack([col_tiles for _ in range(axis_size('tm'))], axis=0)...  70.6 us
    mul x1, local copies, waits for them, and re-layouts, per_device(): return accumulated_sum * factor  48.4 us
    all_gather x1, waiting for transfers between devices, per_device(): col_tiles = lax.all_gather(samples, 'anta', axis=1, tiled=True)  41.4 us
    all_gather x1, waiting for transfers between devices, collect_rows(): return lax.all_gather(own_window, 'antb', axis=0, tiled=True)  34.2 us
    mul x1, other arithmetic, per_device(): return accumulated_sum * factor  23.9 us
    another operation x8, local copies, waits for them, and re-layouts, one_group(): stacked = jnp.stack(pieces, 0)  22.7 us
  transfers between devices with their start and end apart: 3, of which 3 were waited for; matrix products, arithmetic and copies ran while one was open for 1% of the time, Pallas kernels for 0%

profile of v1, /device:TPU:0, one launch (start us, length us, event | category | flops | bytes accessed | tf_op | source)
XLA Modules:
  0.0 626.6 jit_solution(14686554505640058495)
XLA Ops:
  7.3 41.4 %all-gather.3.cloned.1.call-done = bf16[1,512,1536]{2,1,0:T(8,128)(2,1)} async-done(((bf16[1,128,1536]{2,1,0:T(8,128)(2,1)}), bf16[1,512,1536]{2,1,0:T(8,128)(2,1)}) %all-gather.3.cloned.1.call-update) | async-done | bytes 1572880 | tf_op jit(solution)/shard_map/all_gather | solution.py:42
  48.7 4.6 stack.88
  53.3 5.2 all-to-all-start
  58.6 70.6 %all-to-all-done = bf16[4,1,512,1536]{3,2,1,0:T(8,128)(2,1)} async-done(((bf16[4,1,512,1536]{3,2,1,0:T(8,128)(2,1)}), bf16[4,1,512,1536]{3,2,1,0:T(8,128)(2,1)}, u32[]{:S(2)}, u32[]{:S(2)}) %all-to-all-start) | async-done | bytes 6291488 | tf_op jit(solution)/shard_map/all_to_all | solution.py:44
  129.2 8.7 %copy.2 = bf16[4,1,512,1536]{2,3,0,1:T(8,128)(2,1)} copy(bf16[4,1,512,1536]{3,2,1,0:T(8,128)(2,1)} %all-to-all-done) | data formatting | bytes 12582912 | tf_op jit(solution)/shard_map/all_to_all | solution.py:44
  141.0 8.8 %copy.4 = bf16[512,6144]{1,0:T(8,128)(2,1)} copy(bf16[512,6144]{0,1:T(8,128)(2,1)} %bitcast.59) | data formatting | bytes 12582912 | tf_op jit(solution)/shard_map/while | solution.py:26
  149.7 34.2 %all-gather.5.cloned.1.call-done = bf16[2,128,6144]{2,1,0:T(8,128)(2,1)} async-done(((bf16[1,128,6144]{2,1,0:T(8,128)(2,1)}), bf16[2,128,6144]{2,1,0:T(8,128)(2,1)}) %all-gather.5.cloned.1.call-update) | async-done | bytes 3145744 | tf_op jit(solution)/shard_map/all_gather | solution.py:31
  186.1 361.4 %while.14 = (s32[]{:T(128)}, f32[8,8,256,512]{3,2,1,0:T(8,128)}, s32[8]{0:T(128)S(1)}, s32[]{:T(128)}, bf16[256,6400]{1,0:T(8,128)(2,1)S(1)}, /*index=5*/bf16[51...) while((s32[]{:T(128)}, f32[8,8,256,512]{3,2,1,0:T(8,128)}, ...), condition=%wide.region_1.2_spmd, body=%wide.region_0.1_spmd.sunk | while | flops 12884901888 | bytes 85984392 | solution.py:26
  193.2 2.9 bitcast_dynamic-update-slice_fusion.20
  210.2 21.1 %bitcast_dynamic-update-slice_fusion.26 = f32[8,8,256,512]{3,2,1,0:T(8,128)} fusion(f32[8,8,256,512]{3,2,1,0:T(8,128)} %get-tuple-element.222, s32[]{:T(128)} %get-tuple-element.221, bf16[8,256,6144]{2,1,0:T(8,128)(2,1)} %bitcast_dynamic-update-slice_fusion.25, bf16[512,6144]{1,0:T(8,128)(2,1)} %get-tuple-element.251), kind=kOutput, calls=%fused_computation.2.clone.1 | convolution fusion | flops 12884901888 | bytes 35652096 | tf_op jit(solution)/shard_map/while/body/eval_jaxpr/kit,jt->kij/dot_general | solution.py:24
  238.4 2.9 bitcast_dynamic-update-slice_fusion.20
  255.4 21.1 %bitcast_dynamic-update-slice_fusion.26 = f32[8,8,256,512]{3,2,1,0:T(8,128)} fusion(f32[8,8,256,512]{3,2,1,0:T(8,128)} %get-tuple-element.222, s32[]{:T(128)} %get-tuple-element.221, bf16[8,256,6144]{2,1,0:T(8,128)(2,1)} %bitcast_dynamic-update-slice_fusion.25, bf16[512,6144]{1,0:T(8,128)(2,1)} %get-tuple-element.251), kind=kOutput, calls=%fused_computation.2.clone.1 | convolution fusion | flops 12884901888 | bytes 35652096 | tf_op jit(solution)/shard_map/while/body/eval_jaxpr/kit,jt->kij/dot_general | solution.py:24
  283.5 2.9 bitcast_dynamic-update-slice_fusion.20
  300.6 21.1 %bitcast_dynamic-update-slice_fusion.26 = f32[8,8,256,512]{3,2,1,0:T(8,128)} fusion(f32[8,8,256,512]{3,2,1,0:T(8,128)} %get-tuple-element.222, s32[]{:T(128)} %get-tuple-element.221, bf16[8,256,6144]{2,1,0:T(8,128)(2,1)} %bitcast_dynamic-update-slice_fusion.25, bf16[512,6144]{1,0:T(8,128)(2,1)} %get-tuple-element.251), kind=kOutput, calls=%fused_computation.2.clone.1 | convolution fusion | flops 12884901888 | bytes 35652096 | tf_op jit(solution)/shard_map/while/body/eval_jaxpr/kit,jt->kij/dot_general | solution.py:24
  328.7 2.9 bitcast_dynamic-update-slice_fusion.20
  345.7 21.1 %bitcast_dynamic-update-slice_fusion.26 = f32[8,8,256,512]{3,2,1,0:T(8,128)} fusion(f32[8,8,256,512]{3,2,1,0:T(8,128)} %get-tuple-element.222, s32[]{:T(128)} %get-tuple-element.221, bf16[8,256,6144]{2,1,0:T(8,128)(2,1)} %bitcast_dynamic-update-slice_fusion.25, bf16[512,6144]{1,0:T(8,128)(2,1)} %get-tuple-element.251), kind=kOutput, calls=%fused_computation.2.clone.1 | convolution fusion | flops 12884901888 | bytes 35652096 | tf_op jit(solution)/shard_map/while/body/eval_jaxpr/kit,jt->kij/dot_general | solution.py:24
  373.9 2.9 bitcast_dynamic-update-slice_fusion.20
  390.9 21.1 %bitcast_dynamic-update-slice_fusion.26 = f32[8,8,256,512]{3,2,1,0:T(8,128)} fusion(f32[8,8,256,512]{3,2,1,0:T(8,128)} %get-tuple-element.222, s32[]{:T(128)} %get-tuple-element.221, bf16[8,256,6144]{2,1,0:T(8,128)(2,1)} %bitcast_dynamic-update-slice_fusion.25, bf16[512,6144]{1,0:T(8,128)(2,1)} %get-tuple-element.251), kind=kOutput, calls=%fused_computation.2.clone.1 | convolution fusion | flops 12884901888 | bytes 35652096 | tf_op jit(solution)/shard_map/while/body/eval_jaxpr/kit,jt->kij/dot_general | solution.py:24
  436.1 21.1 %bitcast_dynamic-update-slice_fusion.26 = f32[8,8,256,512]{3,2,1,0:T(8,128)} fusion(f32[8,8,256,512]{3,2,1,0:T(8,128)} %get-tuple-element.222, s32[]{:T(128)} %get-tuple-element.221, bf16[8,256,6144]{2,1,0:T(8,128)(2,1)} %bitcast_dynamic-update-slice_fusion.25, bf16[512,6144]{1,0:T(8,128)(2,1)} %get-tuple-element.251), kind=kOutput, calls=%fused_computation.2.clone.1 | convolution fusion | flops 12884901888 | bytes 35652096 | tf_op jit(solution)/shard_map/while/body/eval_jaxpr/kit,jt->kij/dot_general | solution.py:24
  481.3 21.1 %bitcast_dynamic-update-slice_fusion.26 = f32[8,8,256,512]{3,2,1,0:T(8,128)} fusion(f32[8,8,256,512]{3,2,1,0:T(8,128)} %get-tuple-element.222, s32[]{:T(128)} %get-tuple-element.221, bf16[8,256,6144]{2,1,0:T(8,128)(2,1)} %bitcast_dynamic-update-slice_fusion.25, bf16[512,6144]{1,0:T(8,128)(2,1)} %get-tuple-element.251), kind=kOutput, calls=%fused_computation.2.clone.1 | convolution fusion | flops 12884901888 | bytes 35652096 | tf_op jit(solution)/shard_map/while/body/eval_jaxpr/kit,jt->kij/dot_general | solution.py:24
  509.4 2.9 bitcast_dynamic-update-slice_fusion.20
  526.4 21.1 %bitcast_dynamic-update-slice_fusion.26 = f32[8,8,256,512]{3,2,1,0:T(8,128)} fusion(f32[8,8,256,512]{3,2,1,0:T(8,128)} %get-tuple-element.222, s32[]{:T(128)} %get-tuple-element.221, bf16[8,256,6144]{2,1,0:T(8,128)(2,1)} %bitcast_dynamic-update-slice_fusion.25, bf16[512,6144]{1,0:T(8,128)(2,1)} %get-tuple-element.251), kind=kOutput, calls=%fused_computation.2.clone.1 | convolution fusion | flops 12884901888 | bytes 35652096 | tf_op jit(solution)/shard_map/while/body/eval_jaxpr/kit,jt->kij/dot_general | solution.py:24
  547.5 23.9 %broadcast_multiply_fusion = f32[8,8,256,512]{3,2,1,0:T(8,128)} fusion(f32[8,8,256,512]{3,2,1,0:T(8,128)} %get-tuple-element.140), kind=kLoop, calls=%fused_computation.11 | loop fusion | flops 8388608 | bytes 67108864 | tf_op jit(solution)/shard_map/mul | solution.py:58
  571.4 48.4 %mul.39 = f32[64,2,128,1,512]{4,3,2,1,0:T(1,128)} reshape(f32[8,8,256,512]{3,2,1,0:T(8,128)} %broadcast_multiply_fusion) | data formatting | bytes 67108864 | tf_op jit(solution)/shard_map/mul | solution.py:58
  (75 shorter events, 176.0 us)
Async XLA Ops:
  6.5 42.1 %all-gather.3.cloned.1.call-start = ((), (), s32[]{:S(2)}) async-start(), calls=%async_computation.1 | async-start | bytes 1966080 | tf_op jit(solution)/shard_map/all_gather | solution.py:42
  53.3 75.9 %all-to-all-start = ((bf16[4,1,512,1536]{3,2,1,0:T(8,128)(2,1)}), bf16[4,1,512,1536]{3,2,1,0:T(8,128)(2,1)}, u32[]{:S(2)}, u32[]{:S(2)}) async-start(bf16[4,1,512,1536]{3,2,1,0:T(8,128)(2,1)} %stack.88), calls=%async_computation | async-start | bytes 12582912 | tf_op jit(solution)/shard_map/all_to_all | solution.py:44
  58.5 125.5 %all-gather.5.cloned.1.call-start = ((), (), s32[]{:S(2)}) async-start(), calls=%async_computation.2 | async-start | bytes 4718592 | tf_op jit(solution)/shard_map/all_gather | solution.py:31
Sparse Core Ops, SparseCore 0:
  8.9 39.7 all-gather.2
  141.1 42.8 all-gather.4
